TPU v7x, 32 devices: a whole 2x2x4 slice. The times are simulated.
32 devices in a mesh: acq: 8 (over z, y), grp: 4 (over x, core).
Axes of the slice: x: 2, y: 2, z: 4, core: 2. Of those that a mesh axis runs over, the one named last changes fastest.
Arguments:
- tile_slabs: float32 [256, 16, 4096], P(('acq', 'grp')), may hold values from -6 to 6
- dest_rank: int32 [256, 1], replicated, may hold values from 0 to 7; in each aligned block of 8 rows (0 to 7, 8 to 15, ...) at most 2 rows name the same one
- block_slot: int32 [256], replicated, may hold values from 0 to 15
- shifts: float32 [256, 3], replicated, may hold values from 0 to 1
- blend_weight: float32 [256], replicated, may hold values from 0.25 to 4
- parent_map: int32 [512], P(('acq', 'grp')), may hold values from 0 to 63
Outputs:
- pyramid: float32 [64, 8, 8, 1024], P(('acq', 'grp'))
Inputs may be any that keep to these rules, and one draw needn't show every extreme that they name: `dest_rank`: among the rows of one device, no acq index is named more than 2 times, a bound that some block reaches.
All inputs are finite; a program needn't handle non-finite values.
Results may differ from a plain program's by a relative error of at most 0.0003.
Values sent between devices are 32-bit elements; how exact they have to be, the bound alone decides.
A program may use at most 256 MiB of HBM per device.

v0:
```python
import jax
import jax.numpy as jnp
from jax import lax
from jax.sharding import PartitionSpec as P

BZ = 16
BY = 32
BX = 128
PAR_DEV = 2


def resample(blocks, offsets):
    frac_z = offsets[:, 0].reshape(-1, 1, 1, 1)
    frac_y = offsets[:, 1].reshape(-1, 1, 1, 1)
    frac_x = offsets[:, 2].reshape(-1, 1, 1, 1)
    ahead = jnp.concatenate([blocks[:, :, :, 1:], blocks[:, :, :, -1:]], axis=3)
    blocks = (1.0 - frac_x) * blocks + frac_x * ahead
    ahead = jnp.concatenate([blocks[:, :, 1:, :], blocks[:, :, -1:, :]], axis=2)
    blocks = (1.0 - frac_y) * blocks + frac_y * ahead
    ahead = jnp.concatenate([blocks[:, 1:, :, :], blocks[:, -1:, :, :]], axis=1)
    blocks = (1.0 - frac_z) * blocks + frac_z * ahead
    return blocks


def coarsen(blocks):
    count = blocks.shape[0]
    paired = blocks[..., 0::2] + blocks[..., 1::2]
    shaped = paired.reshape(count, BZ // 2, 2, BY // 2, 2, BX // 2)
    summed = jnp.sum(shaped, axis=(2, 4))
    return (0.125 * summed).reshape(count, -1)


def body(tile_slabs, dest_rank, block_slot, shifts, blend_weight, parent_map):
    n_acq = lax.axis_size("acq")
    n_grp = lax.axis_size("grp")
    own_rank = lax.axis_index("acq")
    group_rank = lax.axis_index("grp")
    per_device = tile_slabs.shape[0]
    blocks_dev = parent_map.shape[0]
    capacity_rows = max(2, 2 * per_device // n_acq)
    targets = lax.dynamic_index_in_dim(
        dest_rank[:, 0].reshape(n_acq, n_grp, per_device), group_rank, 1, False
    )
    slots = lax.dynamic_index_in_dim(
        block_slot.reshape(n_acq, n_grp, per_device), group_rank, 1, False
    )
    offsets = lax.dynamic_index_in_dim(
        shifts.reshape(n_acq, n_grp, per_device, 3), group_rank, 1, False
    )
    weights = lax.dynamic_index_in_dim(
        blend_weight.reshape(n_acq, n_grp, per_device), group_rank, 1, False
    )
    owners = jnp.arange(n_acq, dtype=jnp.int32)
    hits = (targets[:, :, None] == owners[None, None, :]).astype(jnp.int32)
    order = jnp.sum((jnp.cumsum(hits, axis=1) - 1) * hits, axis=2)
    own_targets = lax.dynamic_index_in_dim(targets, own_rank, 0, False)
    own_order = lax.dynamic_index_in_dim(order, own_rank, 0, False)
    own_offsets = lax.dynamic_index_in_dim(offsets, own_rank, 0, False)
    send_place = own_targets * capacity_rows + own_order
    send_rows = jnp.arange(n_acq * capacity_rows, dtype=jnp.int32)
    packing = (send_rows[:, None] == send_place[None, :]).astype(jnp.float32)
    capacity = jnp.arange(capacity_rows, dtype=jnp.int32)
    arriving = (
        (targets == own_rank)[:, None, :] & (order[:, None, :] == capacity[None, :, None])
    ).astype(jnp.float32)
    slot_rows = jnp.arange(blocks_dev, dtype=jnp.int32)
    landing = (slots[None, :, :] == slot_rows[:, None, None]).astype(jnp.float32) * weights[
        None, :, :
    ]
    mixing = jnp.einsum("psj,scj->psc", landing, arriving, precision=lax.Precision.HIGHEST).reshape(
        blocks_dev, n_acq * capacity_rows
    )
    denom = jnp.sum(mixing, axis=1)
    local_means = coarsen(resample(tile_slabs.reshape(per_device, BZ, BY, BX), own_offsets))
    sending = jnp.dot(packing, local_means, precision=lax.Precision.HIGHEST)
    received = lax.all_to_all(
        sending.reshape(n_acq, capacity_rows, -1), "acq", split_axis=0, concat_axis=0, tiled=True
    )
    numer = jnp.dot(
        mixing, received.reshape(n_acq * capacity_rows, -1), precision=lax.Precision.HIGHEST
    )
    coarse = numer / jnp.maximum(denom, 1.0)[:, None]
    parent_rows = jnp.arange(n_grp * PAR_DEV * 8, dtype=jnp.int32)
    placing = (parent_rows[:, None] == parent_map[None, :]).astype(jnp.float32)
    partial_value = jnp.dot(placing, coarse, precision=lax.Precision.HIGHEST)
    summed = lax.psum_scatter(partial_value, "grp", scatter_dimension=0, tiled=True)
    return summed.reshape(PAR_DEV, 8, BZ // 2, BY // 2 * (BX // 2))


def solution(mesh):
    placed = (P(("acq", "grp"), None, None), P(), P(), P(), P(), P(("acq", "grp")))
    return jax.shard_map(
        body,
        mesh=mesh,
        in_specs=placed,
        out_specs=P(("acq", "grp"), None, None, None),
        check_vma=False,
    )
```

profile of v0, /device:TPU:1, one launch (start us, length us, event | category | flops | bytes accessed | tf_op | source)
XLA Modules:
  0.0 186.6 jit_solution(11920668778723732026)
XLA Ops:
  6.5 0.8 reshape.98
  7.4 2.0 %copy.26 = f32[16,8,32,128]{3,2,1,0:T(8,128)S(1)} copy(f32[16,8,32,128]{3,1,2,0:T(8,128)} %bitcast.53) | data formatting | bytes 4194304
  9.4 0.6 slice.44
  10.0 0.6 slice.45
  10.6 0.8 fusion.1
  11.4 0.4 slice.46
  11.7 0.1 slice.47
  11.8 0.6 fusion.2
  12.4 0.2 slice.48
  12.7 0.6 fusion.3
  13.3 50.4 %slice.42 = f32[8,16,32,64]{3,2,1,0:T(8,128)} slice(f32[8,16,32,128]{3,2,1,0:T(8,128)S(1)} %fusion.3), slice={[0:8:1], [0:16:1], [0:32:1], [0:128:2]} | slice | bytes 2097152 | tf_op jit(solution)/shard_map/slice | solution.py:27
  63.7 51.2 %slice.43 = f32[8,16,32,64]{3,2,1,0:T(8,128)} slice(f32[8,16,32,128]{3,2,1,0:T(8,128)S(1)} %fusion.3), slice={[0:8:1], [0:16:1], [0:32:1], [1:128:2]} | slice | bytes 2097152 | tf_op jit(solution)/shard_map/slice | solution.py:27
  114.8 2.8 %add.52 = f32[8,16,32,64]{3,2,1,0:T(8,128)S(1)} add(f32[8,16,32,64]{3,2,1,0:T(8,128)} %slice.42, f32[8,16,32,64]{3,2,1,0:T(8,128)} %slice.43) | non-fusion elementwise | flops 262144 | bytes 3145728 | tf_op jit(solution)/shard_map/add | solution.py:27
  117.7 0.0 copy-start.2
  117.7 1.8 reduce_sum.28
  119.5 0.0 copy-start
  119.5 0.0 copy-start.1
  119.6 0.2 reshape.102
  119.7 0.5 broadcast.92
  120.3 0.0 copy-done.2
  120.3 0.7 reduce.5
  120.9 0.1 reshape_squeeze.12
  121.0 0.1 fusion.7
  121.2 0.3 select_reduce_fusion
  121.5 0.4 fusion.17
  121.9 0.0 copy-start.3
  121.9 1.2 copy.20
  123.1 6.4 %all-to-all-start = ((f32[8,2,8192]{2,1,0:T(2,128)}), f32[8,2,8192]{2,1,0:T(2,128)S(1)}, u32[]{:S(2)}, u32[]{:S(2)}) async-start(f32[8,2,8192]{2,1,0:T(2,128)} %copy.20), calls=%async_computation | async-start | bytes 1048576 | tf_op jit(solution)/shard_map/all_to_all | solution.py:76
  129.5 0.0 reduce-scatter.2.cloned.1.call-start
  129.5 0.0 copy-done
  129.5 0.1 reshape.96
  129.6 0.0 copy-done.1
  129.6 0.1 reshape.97
  129.8 0.2 fusion.28
  130.0 12.9 %all-to-all-done = f32[8,2,8192]{2,1,0:T(2,128)S(1)} async-done(((f32[8,2,8192]{2,1,0:T(2,128)}), f32[8,2,8192]{2,1,0:T(2,128)S(1)}, u32[]{:S(2)}, u32[]{:S(2)}) %all-to-all-start) | async-done | bytes 524320 | tf_op jit(solution)/shard_map/all_to_all | solution.py:76
  142.9 0.8 fusion
  143.7 0.0 copy-done.3
  143.7 2.3 %fusion.8 = f32[64,8192]{1,0:T(8,128)} fusion(f32[16,8192]{1,0:T(8,128)S(1)} %fusion, s32[16]{0:T(128)S(1)} %copy-done.3), kind=kOutput, calls=%fused_computation.17 | convolution fusion | flops 100664320 | bytes 2621504 | tf_op jit(solution)/shard_map/dot_general | solution.py:85
  146.1 0.0 reduce-scatter.2.cloned.1.call-update
  146.1 31.5 %reduce-scatter.2.cloned.1.call-done = f32[16,8192]{1,0:T(8,128)} async-done(((f32[64,8192]{1,0:T(8,128)}), f32[16,8192]{1,0:T(8,128)}) %reduce-scatter.2.cloned.1.call-update) | async-done | bytes 524304 | tf_op jit(solution)/shard_map/reduce_scatter | solution.py:86
  177.6 2.1 %copy.23 = f32[2,8,8,1024]{3,2,1,0:T(8,128)} copy(f32[2,8,8,1024]{3,1,2,0:T(8,128)} %bitcast.54) | data formatting | bytes 1048576 | tf_op jit(solution)/shard_map/reshape | solution.py:87
  (14 shorter events, 0.2 us)
Async XLA Ops:
  117.7 2.6 %copy-start.2 = (s32[256,1]{0,1:T(1,128)S(1)}, s32[256,1]{0,1:T(1,128)}, u32[]{:S(2)}) copy-start(s32[256,1]{0,1:T(1,128)} %param.7) | copy-start | bytes 3076
  119.5 10.0 %copy-start = (s32[256]{0:T(256)S(1)}, s32[256]{0:T(256)}, u32[]{:S(2)}) copy-start(s32[256]{0:T(256)} %param.8) | copy-start | bytes 3076
  119.5 10.1 %copy-start.1 = (f32[256]{0:T(256)S(1)}, f32[256]{0:T(256)}, u32[]{:S(2)}) copy-start(f32[256]{0:T(256)} %param.10) | copy-start | bytes 3076
  121.9 21.8 %copy-start.3 = (s32[16]{0:T(128)S(1)}, s32[16]{0:T(128)}, u32[]{:S(2)}) copy-start(s32[16]{0:T(128)} %param.11) | copy-start | bytes 196
  123.1 19.8 %all-to-all-start = ((f32[8,2,8192]{2,1,0:T(2,128)}), f32[8,2,8192]{2,1,0:T(2,128)S(1)}, u32[]{:S(2)}, u32[]{:S(2)}) async-start(f32[8,2,8192]{2,1,0:T(2,128)} %copy.20), calls=%async_computation | async-start | bytes 1048576 | tf_op jit(solution)/shard_map/all_to_all | solution.py:76
  129.5 48.1 %reduce-scatter.2.cloned.1.call-start = ((), (), s32[]{:S(2)}) async-start(), calls=%async_computation.2 | async-start | bytes 2621440 | tf_op jit(solution)/shard_map/reduce_scatter | solution.py:86
Sparse Core Ops, SparseCore 0:
  146.2 31.3 reduce-scatter.1
where the time goes:
time: 188 us; the launch traced here: 187 us
  local copies, waits for them, and re-layouts  111 us (59%)
  waiting for transfers between devices  44.4 us (24%)
  between operations  13.7 us (7%)
  other arithmetic  7.7 us (4%)
  starting transfers between devices  6.41 us (3%)
  matrix products  3.8 us (2%)
    slice x2, local copies, waits for them, and re-layouts, coarsen(): paired = blocks[..., 0::2] + blocks[..., 1::2]  102 us
    reduce_scatter x1, waiting for transfers between devices, body(): lax.psum_scatter(partial_value, 'grp', scatter_dimension=0, tiled=True)  31.5 us
    all_to_all x1, waiting for transfers between devices, body(): lax.all_to_all(sending.reshape(n_acq, capacity_rows, -1), 'acq', split_ax...  12.9 us
    all_to_all x1, starting transfers between devices, body(): lax.all_to_all(sending.reshape(n_acq, capacity_rows, -1), 'acq', split_ax...  6.37 us
  transfers between devices with their start and end apart: 2, of which 2 were waited for; matrix products, arithmetic and copies ran while one was open for 0% of the time, Pallas kernels for 0%

commit v1 on v0

v1 whole, which is shorter than its diff:
```python
import functools
import jax
import jax.numpy as jnp
from jax import lax
from jax.experimental import pallas as pl
from jax.experimental.pallas import tpu as pltpu
from jax.sharding import PartitionSpec as P

BZ = 16
BY = 32
BX = 128
PAR_DEV = 2
HZ, HY, HX = BZ // 2, BY // 2, BX // 2
PAIRS = HY // 2
LANES = HY * HX
MESH = pl.DeviceIdType.MESH


def flip(index, mask, count):
    if count & (count - 1):
        return (2 * count + mask - index) % count
    out, bit = index, 1
    while bit < count:
        if mask & bit:
            out = out + bit * (1 - 2 * ((index // bit) % 2))
        bit *= 2
    return out


def partners(count):
    return list(range(1, count)) if count & (count - 1) == 0 else list(range(count))


def halving_matrix():
    row = lax.broadcasted_iota(jnp.int32, (2 * BX, 2 * BX), 0)
    col = lax.broadcasted_iota(jnp.int32, (2 * BX, 2 * BX), 1)
    x, y = row % BX, row // BX
    cx, cy, part = col % HX, (col // HX) % 2, col // BX
    same = y == cy
    both = jnp.where(same & (x // 2 == cx), 1.0, 0.0)
    ahead = jnp.where(same & (x == jnp.minimum(2 * cx + 2, BX - 1)), 1.0, 0.0)
    here = jnp.where(same & (x == 2 * cx), 1.0, 0.0)
    return jnp.where(part == 0, both, ahead - here).astype(jnp.bfloat16)


def split(values):
    high = values.astype(jnp.bfloat16)
    return high, (values - high.astype(jnp.float32)).astype(jnp.bfloat16)


def kernel(
    n_acq, n_grp, cap, scal, source, tile_hbm, slot_lane, parents, out,
    tile, thin, high, low, half, send, gath, pmap,
    load_sem, send_a, recv_a, send_x, recv_x, send_c, recv_c, send_p, recv_p,
):
    count = tile.shape[0]
    a, g = lax.axis_index("acq"), lax.axis_index("grp")
    hi, lo = g // 2, g % 2
    mate = hi * 2 + (1 - lo)
    n_hi = n_grp // 2
    rows = PAIRS * HZ

    barrier = pltpu.get_barrier_semaphore()
    for d in range(1, n_acq):
        pl.semaphore_signal(barrier, inc=1, device_id=((a + d) % n_acq, g), device_id_type=MESH)
    for d in range(1, n_grp):
        pl.semaphore_signal(barrier, inc=1, device_id=(a, (g + d) % n_grp), device_id_type=MESH)

    loads = [pltpu.make_async_copy(tile_hbm.at[s], tile.at[s], load_sem.at[s]) for s in range(count)]
    for load in loads:
        load.start()

    matrix = halving_matrix()
    last = lax.broadcasted_iota(jnp.int32, (HZ, BX), 0) == HZ - 1

    def soften(s, carry):
        pltpu.make_async_copy(tile_hbm.at[s], tile.at[s], load_sem.at[s]).wait()
        fz, fy = scal[s, 0], scal[s, 1]

        def row(y):
            return tile[s, :, pl.ds(y * BX, BX)]

        here = row(0)
        for j in range(HY):
            odd = row(2 * j + 1)
            ahead = row(2 * j + 2) if j < HY - 1 else odd
            thin[s, j] = here + odd + fy * (ahead - here)
            here = ahead
        for j in range(HY):
            even = thin[s, j, pl.ds(0, HZ, stride=2), :]
            odd = thin[s, j, pl.ds(1, HZ, stride=2), :]
            ahead = jnp.where(last, odd, pltpu.roll(even, HZ - 1, 0))
            top, rest = split(even + odd + fz * (ahead - even))
            place = (pl.ds((j // 2) * HZ, HZ), pl.ds((j % 2) * BX, BX))
            high[s, place[0], place[1]] = top.astype(jnp.float32)
            low[s, place[0], place[1]] = rest.astype(jnp.float32)
        return carry

    lax.fori_loop(0, count, soften, 0)

    def halve(s, carry):
        half[s] = jnp.dot(
            high[s].astype(jnp.bfloat16), matrix, preferred_element_type=jnp.float32
        ) + jnp.dot(low[s].astype(jnp.bfloat16), matrix, preferred_element_type=jnp.float32)
        return carry

    lax.fori_loop(0, count, halve, 0, unroll=True)
    half[count] = jnp.zeros((rows, 2 * BX), jnp.float32)

    for place in range(n_acq * cap):
        s = source[place]
        fx, weight = scal[s, 2], scal[s, 3]
        value = weight * (half[s, :, pl.ds(0, BX)] + fx * half[s, :, pl.ds(BX, BX)])
        for p in range(PAIRS):
            send[place // cap, pl.ds((place % cap) * HZ, HZ), pl.ds(p * BX, BX)] = value[
                p * HZ : (p + 1) * HZ
            ]

    pl.semaphore_wait(barrier, n_acq - 1 + n_grp - 1)

    def to_acq(peer):
        return pltpu.make_async_remote_copy(
            src_ref=send.at[peer], dst_ref=gath.at[g, a],
            send_sem=send_a.at[peer], recv_sem=recv_a.at[a],
            device_id=(peer, g), device_id_type=MESH,
        )

    def from_acq(peer):
        return pltpu.make_async_remote_copy(
            src_ref=send.at[peer], dst_ref=gath.at[g, peer],
            send_sem=send_a.at[peer], recv_sem=recv_a.at[peer],
            device_id=(peer, g), device_id_type=MESH,
        )

    def across(owner, k, peer, sends, recvs, at):
        return pltpu.make_async_remote_copy(
            src_ref=gath.at[owner, k], dst_ref=gath.at[owner, k],
            send_sem=sends.at[at, k], recv_sem=recvs.at[owner, k],
            device_id=(a, peer), device_id_type=MESH,
        )

    gath[g, a] = send[a]
    pmap[g] = parents[...]
    order = [flip(a, d, n_acq) for d in range(1, n_acq)]
    for peer in order:
        to_acq(peer).start()
    for d in range(1, n_grp):
        peer = (g + d) % n_grp
        pltpu.make_async_remote_copy(
            src_ref=parents, dst_ref=pmap.at[g], send_sem=send_p.at[d], recv_sem=recv_p.at[g],
            device_id=(a, peer), device_id_type=MESH,
        ).start()

    others = [((hi + d) % n_hi) * 2 + lo for d in range(1, n_hi)]
    origins = [((hi + n_hi - d) % n_hi) * 2 + lo for d in range(1, n_hi)]
    mates = [mate] + [((hi + n_hi - d) % n_hi) * 2 + 1 - lo for d in range(1, n_hi)]

    def forward(k):
        for d, peer in enumerate(others):
            across(g, k, peer, send_x, recv_x, d).start()
        across(g, k, mate, send_c, recv_c, 0).start()

    def relay(k):
        for d, owner in enumerate(origins):
            across(owner, k, mate, send_x, recv_x, d).wait_recv()
            across(owner, k, mate, send_c, recv_c, d + 1).start()

    steps = [a] + order
    for i, k in enumerate(steps):
        if i > 0:
            from_acq(k).wait_recv()
        forward(k)
        if i > 0:
            relay(steps[i - 1])
    relay(steps[-1])

    for d in range(1, n_grp):
        peer = (g + n_grp - d) % n_grp
        pltpu.make_async_remote_copy(
            src_ref=parents, dst_ref=pmap.at[peer], send_sem=send_p.at[d], recv_sem=recv_p.at[peer],
            device_id=(a, peer), device_id_type=MESH,
        ).wait_recv()
    for owner in mates:
        for k in steps:
            across(owner, k, mate, send_c, recv_c, 0).wait_recv()

    depth = n_acq * cap * HZ
    tall = PAR_DEV * 8 * HZ
    lane = lax.broadcasted_iota(jnp.int32, (1, depth), 1)
    spot = lax.broadcasted_iota(jnp.int32, (tall, depth), 0) + g * tall
    blocks = pmap.shape[1]
    places = lax.broadcasted_iota(jnp.int32, (blocks, depth), 0)
    total = None
    for owner in range(n_grp):
        named = jnp.sum(
            jnp.where(slot_lane[pl.ds(owner, 1), :] == places, pmap[owner], 0), axis=0, keepdims=True
        )
        placing = jnp.where(named * HZ + lane % HZ == spot, 1.0, 0.0).astype(jnp.bfloat16)
        top, rest = split(gath[owner].reshape(depth, LANES))
        part = jnp.dot(placing, top, preferred_element_type=jnp.float32) + jnp.dot(
            placing, rest, preferred_element_type=jnp.float32
        )
        total = part if total is None else total + part
    out[...] = total

    for peer in order:
        to_acq(peer).wait_send()
    for d in range(1, n_grp):
        pltpu.make_async_remote_copy(
            src_ref=parents, dst_ref=pmap.at[g], send_sem=send_p.at[d], recv_sem=recv_p.at[g],
            device_id=(a, (g + d) % n_grp), device_id_type=MESH,
        ).wait_send()
    for k in steps:
        for d, peer in enumerate(others):
            across(g, k, peer, send_x, recv_x, d).wait_send()
        across(g, k, mate, send_c, recv_c, 0).wait_send()
        for d, owner in enumerate(origins):
            across(owner, k, mate, send_c, recv_c, d + 1).wait_send()


def body(tile_slabs, dest_rank, block_slot, shifts, blend_weight, parent_map):
    n_acq, n_grp = lax.axis_size("acq"), lax.axis_size("grp")
    a, g = lax.axis_index("acq"), lax.axis_index("grp")
    count = tile_slabs.shape[0]
    blocks = parent_map.shape[0]
    cap = max(2, 2 * count // n_acq)
    shape = (n_acq, n_grp, count)

    def mine(values):
        return lax.dynamic_index_in_dim(values.reshape(shape), g, 1, False)

    dest, slots = dest_rank[:, 0].reshape(shape), block_slot.reshape(shape)
    targets, places, weights = mine(dest), mine(slots), mine(blend_weight)
    own = a * n_grp + g
    offsets = lax.dynamic_index_in_dim(shifts.reshape(n_acq * n_grp, count, 3), own, 0, False)
    own_target = lax.dynamic_index_in_dim(targets, a, 0, False)
    own_place = lax.dynamic_index_in_dim(places, a, 0, False)
    own_weight = lax.dynamic_index_in_dim(weights, a, 0, False)
    key = (targets * blocks + places).reshape(1, -1)
    own_key = (own_target * blocks + own_place).reshape(-1, 1)
    denom = jnp.sum(jnp.where(key == own_key, weights.reshape(1, -1), 0.0), axis=1)
    factor = 0.125 * own_weight / jnp.maximum(denom, 1.0)
    scal = jnp.concatenate([offsets, factor[:, None]], axis=1)
    scal = jnp.concatenate([scal, jnp.zeros((1, 4), jnp.float32)], axis=0)

    index = jnp.arange(count, dtype=jnp.int32)
    earlier = index[None, :] < index[:, None]
    own_order = jnp.sum(
        ((own_target[None, :] == own_target[:, None]) & earlier).astype(jnp.int32), axis=1
    )
    spot = own_target * cap + own_order
    send_rows = jnp.arange(n_acq * cap, dtype=jnp.int32)
    source = count - jnp.sum(
        jnp.where(send_rows[:, None] == spot[None, :], count - index[None, :], 0), axis=1
    )

    here = dest == a
    order = jnp.sum((here[:, :, None, :] & earlier).astype(jnp.int32), axis=3)
    capacity = jnp.arange(cap, dtype=jnp.int32)
    arriving = here[:, :, None, :] & (order[:, :, None, :] == capacity[:, None])
    slot_of = jnp.sum(jnp.where(arriving, slots[:, :, None, :] + 1, 0), axis=3) - 1
    depth = n_acq * cap * HZ
    slot_lane = jnp.repeat(slot_of.transpose(1, 0, 2).reshape(n_grp, n_acq * cap), HZ, axis=1)
    parents = jnp.broadcast_to(parent_map[:, None], (blocks, depth))

    vmem, smem = pl.BlockSpec(memory_space=pltpu.VMEM), pl.BlockSpec(memory_space=pltpu.SMEM)
    rows = PAIRS * HZ
    dma = pltpu.SemaphoreType.DMA
    n_hi = n_grp // 2
    summed = pl.pallas_call(
        functools.partial(kernel, n_acq, n_grp, cap),
        out_shape=jax.ShapeDtypeStruct((PAR_DEV * 8 * HZ, LANES), jnp.float32),
        in_specs=[smem, smem, pl.BlockSpec(memory_space=pl.ANY), vmem, vmem],
        out_specs=vmem,
        scratch_shapes=[
            pltpu.VMEM((count, BZ, BY * BX), jnp.float32),
            pltpu.VMEM((count, HY, BZ, BX), jnp.float32),
            pltpu.VMEM((count, rows, 2 * BX), jnp.float32),
            pltpu.VMEM((count, rows, 2 * BX), jnp.float32),
            pltpu.VMEM((count + 1, rows, 2 * BX), jnp.float32),
            pltpu.VMEM((n_acq, cap * HZ, LANES), jnp.float32),
            pltpu.VMEM((n_grp, n_acq, cap * HZ, LANES), jnp.float32),
            pltpu.VMEM((n_grp, blocks, depth), jnp.int32),
            dma((count,)),
            dma((n_acq,)), dma((n_acq,)),
            dma((max(1, n_hi - 1), n_acq)), dma((n_grp, n_acq)),
            dma((n_hi, n_acq)), dma((n_grp, n_acq)),
            dma((n_grp,)), dma((n_grp,)),
        ],
        compiler_params=pltpu.CompilerParams(collective_id=0, has_side_effects=True),
    )(scal, source, tile_slabs, slot_lane, parents)
    return summed.reshape(PAR_DEV, 8, HZ, LANES)


def solution(mesh):
    placed = (P(("acq", "grp"), None, None), P(), P(), P(), P(), P(("acq", "grp")))
    return jax.shard_map(
        body,
        mesh=mesh,
        in_specs=placed,
        out_specs=P(("acq", "grp"), None, None, None),
        check_vma=False,
    )
```

time: 188 us -> 40.2 us (0.21)
  local copies, waits for them, and re-layouts: 111 us -> 7.5 us
  waiting for transfers between devices: 44.4 us -> 0 us
  Pallas kernels: 0 us -> 28.3 us
  between operations: 13.7 us -> 0.12 us
  starting transfers between devices: 6.41 us -> 0 us
  matrix products: 3.8 us -> 0 us
  other arithmetic: 7.7 us -> 4.01 us
    slice x8 -> x0, local copies, waits for them, and re-layouts: 103 us -> none  [the longest x2 102 us: coarsen(): paired = blocks[..., 0::2] + blocks[..., 1::2]]
    reduce_scatter x1 -> x0, waiting for transfers between devices: 31.5 us -> none  [body(): lax.psum_scatter(partial_value, 'grp', scatter_dimension=0, tiled=True)]
    pallas_call x0 -> x1, Pallas kernels: none -> 28.3 us  [body(): pl.pallas_call(functools.partial(kernel, n_acq, n_grp, cap), out_shape=ja...]
    all_to_all x1 -> x0, waiting for transfers between devices: 12.9 us -> none  [body(): lax.all_to_all(sending.reshape(n_acq, capacity_rows, -1), 'acq', split_ax...]
    all_to_all x1 -> x0, starting transfers between devices: 6.37 us -> none  [body(): lax.all_to_all(sending.reshape(n_acq, capacity_rows, -1), 'acq', split_ax...]
    add x4 -> x3, other arithmetic: 4.77 us -> 0.05 us  [the longest x1 0.03 us: body(): key = (targets * blocks + places).reshape(1, -1)]
    dot_general x4 -> x0, matrix products: 3.8 us -> none  [the longest x1 2.32 us: body(): partial_value = jnp.dot(placing, coarse, precision=lax.Precision.HIGHEST)]
  transfers between devices with their start and end apart: 2 -> 0, of which waited for: 2 -> 0; matrix products, arithmetic and copies ran while one was open for 0% -> 0% of each run, Pallas kernels for 0% -> 0%
where the time goes in v1:
time: 40.2 us; the launch traced here: 39.9 us
  Pallas kernels  28.3 us (70%)
  local copies, waits for them, and re-layouts  7.5 us (19%)
  other arithmetic  4.01 us (10%)
    pallas_call x1, Pallas kernels, body(): pl.pallas_call(functools.partial(kernel, n_acq, n_grp, cap), out_shape=ja...  28.3 us
    unnamed x2, local copies, waits for them, and re-layouts  2.4 us
    unnamed x1, other arithmetic  1.34 us
    broadcast_in_dim x1, local copies, waits for them, and re-layouts, body(): parents = jnp.broadcast_to(parent_map[:, None], (blocks, depth))  1.32 us

profile of v1, /device:TPU:1, one launch (start us, length us, event | category | flops | bytes accessed | tf_op | source)
XLA Modules:
  0.0 39.9 jit_solution(17300852759867359926)
XLA Ops:
  0.0 0.5 %broadcast.109 = s32[]{:T(128)} broadcast(s32[]{:T(128)} %constant.96.clone.1), dimensions={} | broadcast | bytes 8 | tf_op args[1]
  0.5 1.3 %reduce.11 = s32[256]{0:T(256)S(1)} reduce(s32[256,1]{0,1:T(1,128)} %param.7, s32[]{:T(128)} %broadcast.109), dimensions={1}, to_apply=%param.7.reduce_sub_computation.3 | reduce | bytes 2052 | tf_op args[1]
  1.9 1.3 %broadcast_in_dim.67.parents = s32[16,128]{1,0:T(8,128)} broadcast(s32[16]{0:T(128)} %param.11), dimensions={0} | broadcast | bytes 8256 | tf_op jit(solution)/shard_map/broadcast_in_dim | solution.py:264
  3.2 0.1 reshape_squeeze.3
  3.3 0.6 %convert_reduce_fusion = s32[8,4,8]{2,1,0:T(4,128)S(1)} fusion(pred[8,8]{1,0:T(8,128)(4,1)S(1)} %iota_compare_fusion.2, pred[8,4,8]{2,1,0:T(4,128)(4,1)S(1)} %bitcast.24), kind=kLoop, calls=%fused_computation | loop fusion | flops 5888 | bytes 1344 | tf_op jit(solution)/shard_map/reduce_sum | solution.py:258
  4.0 0.8 %reshape.120 = s32[8,4,8]{2,1,0:T(4,128)S(1)} reshape(s32[256]{0:T(256)} %param.8) | data formatting | bytes 2048 | tf_op jit(solution)/shard_map/reshape | solution.py:232
  4.8 0.1 add.75
  4.9 0.2 select_reduce_fusion
  5.1 0.2 convert_reduce_fusion.1
  5.3 0.1 select_reduce_fusion.1
  5.4 0.6 %broadcast_subtract_fusion.source = s32[16]{0:T(128)} fusion(s32[16]{0:T(128)S(1)} %select_reduce_fusion.1), kind=kLoop, calls=%fused_computation.28 | loop fusion | flops 16 | bytes 128 | tf_op jit(solution)/shard_map/sub | solution.py:253
  6.0 0.1 copy.22
  6.1 0.1 copy.23
  6.2 0.8 %reshape.119 = f32[8,4,8]{2,1,0:T(4,128)S(1)} reshape(f32[256]{0:T(256)} %param.10) | data formatting | bytes 2048 | tf_op jit(solution)/shard_map/reshape | solution.py:230
  7.0 0.1 broadcast_in_dim.59
  7.1 0.2 select_reduce_fusion.2
  7.3 0.1 copy.17
  7.3 0.1 copy.16
  7.4 0.1 broadcast_in_dim.66
  7.5 0.7 %reshape.122.slot_lane = s32[4,128]{1,0:T(4,128)} reshape(s32[4,16,8]{2,1,0:T(8,128)S(1)} %broadcast_in_dim.66) | data formatting | bytes 4096 | tf_op jit(solution)/shard_map/reshape | solution.py:263
  8.2 0.8 %reshape.118 = f32[32,8,3]{1,0,2:T(8,128)S(1)} reshape(f32[256,3]{0,1:T(4,128)} %param.9) | data formatting | bytes 6144 | tf_op jit(solution)/shard_map/reshape | solution.py:235
  9.0 0.1 copy.24
  9.1 0.7 %select_maximum_fusion.scal = f32[9,4]{1,0:T(8,128)} fusion(f32[8,1]{1,0:T(8,128)S(1)} %div.10, f32[8,3]{1,0:T(8,128)S(1)} %bitcast.26), kind=kLoop, calls=%fused_computation.4 | loop fusion | flops 144 | bytes 272 | tf_op jit(solution)/shard_map/concatenate | solution.py:243
  9.7 28.3 %shard_map.64 = f32[128,1024]{1,0:T(8,128)} custom-call(f32[9,4]{1,0:T(8,128)} %select_maximum_fusion.scal, s32[16]{0:T(128)} %broadcast_subtract_fusion.source, f32[8,16,4096]{2,1,0:T(8,128)} %tile_hbm.1, s32[4,128]{1,0:T(4,128)} %reshape.122.slot_lane, s32[16,128]{1,0:T(8,128)} %broadcast_in_dim.67.parents), custom_call_target="tpu_custom_call" | custom-call | tf_op jit(solution)/shard_map/pallas_call | solution.py:270
  38.0 1.9 %copy.26 = f32[2,8,8,1024]{3,2,1,0:T(8,128)} copy(f32[2,8,8,1024]{3,2,1,0:T(8,128)} %bitcast.21) | data formatting | bytes 1048576
  (15 shorter events, 0.1 us)

commit v2 on v1

v2 whole, which is shorter than its diff:
```python
import functools
import jax
import jax.numpy as jnp
from jax import lax
from jax.experimental import pallas as pl
from jax.experimental.pallas import tpu as pltpu
from jax.sharding import PartitionSpec as P

BZ = 16
BY = 32
BX = 128
PAR_DEV = 2
HZ, HY, HX = BZ // 2, BY // 2, BX // 2
PAIRS = HY // 2
LANES = HY * HX
VMEM_LIMIT = 62
MESH = pl.DeviceIdType.MESH


def flip(index, mask, count):
    if count & (count - 1):
        return (2 * count + mask - index) % count
    out, bit = index, 1
    while bit < count:
        if mask & bit:
            out = out + bit * (1 - 2 * ((index // bit) % 2))
        bit *= 2
    return out


def partners(count):
    return list(range(1, count)) if count & (count - 1) == 0 else list(range(count))


def halving_matrix():
    row = lax.broadcasted_iota(jnp.int32, (2 * BX, 2 * BX), 0)
    col = lax.broadcasted_iota(jnp.int32, (2 * BX, 2 * BX), 1)
    x, y = row % BX, row // BX
    cx, cy, part = col % HX, (col // HX) % 2, col // BX
    same = y == cy
    both = jnp.where(same & (x // 2 == cx), 1.0, 0.0)
    ahead = jnp.where(same & (x == jnp.minimum(2 * cx + 2, BX - 1)), 1.0, 0.0)
    here = jnp.where(same & (x == 2 * cx), 1.0, 0.0)
    return jnp.where(part == 0, both, ahead - here).astype(jnp.bfloat16)


def split(values):
    high = values.astype(jnp.bfloat16)
    return high, (values - high.astype(jnp.float32)).astype(jnp.bfloat16)


def kernel(
    n_acq, n_grp, cap, tile_hbm, dest_hbm, slot_hbm, weight_hbm, shift_hbm, parent_hbm, out,
    dest, slot, weight, shift, parent, dest_row, slot_row, weight_row,
    tile, thin, high, low, half, factor, send, gath, named,
    meta_sem, load_sem, send_a, recv_a, send_x, recv_x, send_c, recv_c, send_p, recv_p,
):
    count = tile.shape[0]
    a, g = lax.axis_index("acq"), lax.axis_index("grp")
    hi, lo = g // 2, g % 2
    mate = hi * 2 + (1 - lo)
    n_hi = n_grp // 2
    rows = PAIRS * HZ

    barrier = pltpu.get_barrier_semaphore()
    for d in range(1, n_acq):
        pl.semaphore_signal(barrier, inc=1, device_id=((a + d) % n_acq, g), device_id_type=MESH)
    for d in range(1, n_grp):
        pl.semaphore_signal(barrier, inc=1, device_id=(a, (g + d) % n_grp), device_id_type=MESH)

    metas = [
        pltpu.make_async_copy(start, end, meta_sem.at[i])
        for i, (start, end) in enumerate((
            (dest_hbm, dest), (slot_hbm, slot), (weight_hbm, weight), (shift_hbm, shift),
            (parent_hbm, parent), (dest_hbm, dest_row), (slot_hbm, slot_row), (weight_hbm, weight_row),
        ))
    ]
    for meta in metas:
        meta.start()
    loads = [pltpu.make_async_copy(tile_hbm.at[s], tile.at[s], load_sem.at[s]) for s in range(count)]
    for load in loads:
        load.start()

    matrix = halving_matrix()
    last = lax.broadcasted_iota(jnp.int32, (HZ, BX), 0) == HZ - 1
    for meta in metas:
        meta.wait()

    blocks = parent.shape[1]
    base = (a * n_grp + g) * count
    target = [dest[0, base + s] for s in range(count)]
    key = [target[s] * blocks + slot[0, base + s] for s in range(count)]
    subs = lax.broadcasted_iota(jnp.int32, dest_row.shape, 1)
    keys = jnp.where(
        (subs // count) % n_grp == g, dest_row[...] * blocks + slot_row[...], -1
    )
    for s in range(count):
        denom = jnp.sum(jnp.where(keys == key[s], weight_row[...], 0.0), axis=1, keepdims=True)
        factor[s] = jnp.broadcast_to(
            (0.125 * weight[0, base + s]) / jnp.maximum(denom, 1.0), (HZ, BX)
        )
    factor[count] = jnp.zeros((HZ, BX), jnp.float32)
    spot = []
    for s in range(count):
        at = target[s] * cap
        for before in range(s):
            at = at + jnp.where(target[before] == target[s], 1, 0)
        spot.append(at)

    def soften(s, carry):
        pltpu.make_async_copy(tile_hbm.at[s], tile.at[s], load_sem.at[s]).wait()
        fz, fy = shift[0, base + s], shift[1, base + s]

        def row(y):
            return tile[s, :, pl.ds(y * BX, BX)]

        here = row(0)
        for j in range(HY):
            odd = row(2 * j + 1)
            ahead = row(2 * j + 2) if j < HY - 1 else odd
            thin[s, j] = here + odd + fy * (ahead - here)
            here = ahead
        for j in range(HY):
            even = thin[s, j, pl.ds(0, HZ, stride=2), :]
            odd = thin[s, j, pl.ds(1, HZ, stride=2), :]
            ahead = jnp.where(last, odd, pltpu.roll(even, HZ - 1, 0))
            top, rest = split(even + odd + fz * (ahead - even))
            place = (pl.ds((j // 2) * HZ, HZ), pl.ds((j % 2) * BX, BX))
            high[s, place[0], place[1]] = top.astype(jnp.float32)
            low[s, place[0], place[1]] = rest.astype(jnp.float32)
        return carry

    lax.fori_loop(0, count, soften, 0)

    def halve(s, carry):
        half[s] = jnp.dot(
            high[s].astype(jnp.bfloat16), matrix, preferred_element_type=jnp.float32
        ) + jnp.dot(low[s].astype(jnp.bfloat16), matrix, preferred_element_type=jnp.float32)
        return carry

    lax.fori_loop(0, count, halve, 0, unroll=True)
    half[count] = jnp.zeros((rows, 2 * BX), jnp.float32)

    for place in range(n_acq * cap):
        s = count
        for i in range(count):
            s = jnp.where(spot[i] == place, i, s)
        fx = shift[2, base + jnp.minimum(s, count - 1)]
        value = half[s, :, pl.ds(0, BX)] + fx * half[s, :, pl.ds(BX, BX)]
        scale = factor[s]
        for p in range(PAIRS):
            send[place // cap, pl.ds((place % cap) * HZ, HZ), pl.ds(p * BX, BX)] = scale * value[
                p * HZ : (p + 1) * HZ
            ]

    pl.semaphore_wait(barrier, n_acq - 1 + n_grp - 1)

    def to_acq(peer):
        return pltpu.make_async_remote_copy(
            src_ref=send.at[peer], dst_ref=gath.at[g, a],
            send_sem=send_a.at[peer], recv_sem=recv_a.at[a],
            device_id=(peer, g), device_id_type=MESH,
        )

    def from_acq(peer):
        return pltpu.make_async_remote_copy(
            src_ref=send.at[peer], dst_ref=gath.at[g, peer],
            send_sem=send_a.at[peer], recv_sem=recv_a.at[peer],
            device_id=(peer, g), device_id_type=MESH,
        )

    def across(owner, k, peer, sends, recvs, at):
        return pltpu.make_async_remote_copy(
            src_ref=gath.at[owner, k], dst_ref=gath.at[owner, k],
            send_sem=sends.at[at, k], recv_sem=recvs.at[owner, k],
            device_id=(a, peer), device_id_type=MESH,
        )

    gath[g, a] = send[a]
    order = [flip(a, d, n_acq) for d in partners(n_acq)]
    for peer in order:
        to_acq(peer).start()

    others = [((hi + d) % n_hi) * 2 + lo for d in range(1, n_hi)]
    origins = [((hi + n_hi - d) % n_hi) * 2 + lo for d in range(1, n_hi)]
    mates = [mate] + [((hi + n_hi - d) % n_hi) * 2 + 1 - lo for d in range(1, n_hi)]

    def forward(k):
        for d, peer in enumerate(others):
            across(g, k, peer, send_x, recv_x, d).start()
        across(g, k, mate, send_c, recv_c, 0).start()

    def relay(k):
        for d, owner in enumerate(origins):
            across(owner, k, mate, send_x, recv_x, d).wait_recv()
            across(owner, k, mate, send_c, recv_c, d + 1).start()

    depth = n_acq * cap * HZ
    tall = PAR_DEV * 8 * HZ
    lane = lax.broadcasted_iota(jnp.int32, (HZ, depth), 1)

    def name(k, found):
        first = (k * n_grp + g) * count
        seen = 0
        slots = [0] * cap
        for s in range(count):
            hit = jnp.where(dest[0, first + s] == a, 1, 0)
            for c in range(cap):
                slots[c] = jnp.where(
                    (hit == 1) & (seen == c), slot[0, first + s], slots[c]
                )
            seen = seen + hit
        for c in range(cap):
            found = jnp.where(lane // HZ == k * cap + c, parent[0, slots[c]], found)
        return found

    steps = [a] + order
    forward(a)
    named[g] = lax.fori_loop(0, n_acq, name, jnp.zeros((HZ, depth), jnp.int32))

    def telling(d, owner, peer):
        return pltpu.make_async_remote_copy(
            src_ref=named.at[owner], dst_ref=named.at[owner],
            send_sem=send_p.at[d], recv_sem=recv_p.at[owner],
            device_id=(a, peer), device_id_type=MESH,
        )

    for d in range(1, n_grp):
        telling(d, g, (g + d) % n_grp).start()

    upright = lax.broadcasted_iota(jnp.int32, (tall, depth), 0) + g * tall
    across_lane = lax.broadcasted_iota(jnp.int32, (tall, depth), 1) % HZ

    def place_rows(owner):
        placing = jnp.where(
            named[owner, pl.ds(0, 1), :] * HZ + across_lane == upright, 1.0, 0.0
        ).astype(jnp.bfloat16)
        top, rest = split(gath[owner].reshape(depth, LANES))
        return jnp.dot(placing, top, preferred_element_type=jnp.float32) + jnp.dot(
            placing, rest, preferred_element_type=jnp.float32
        )

    for i in range(1, n_acq):
        from_acq(steps[i]).wait_recv()
        forward(steps[i])
        relay(steps[i - 1])
    out[...] = place_rows(g)
    for d in range(1, n_grp):
        owner = (g + n_grp - d) % n_grp
        telling(d, owner, owner).wait_recv()
    for k in steps:
        across(mate, k, mate, send_c, recv_c, 0).wait_recv()
    out[...] += place_rows(mate)
    relay(steps[-1])
    for owner in origins:
        out[...] += place_rows(owner)
    for owner in mates[1:]:
        for k in steps:
            across(owner, k, mate, send_c, recv_c, 0).wait_recv()
        out[...] += place_rows(owner)

    for peer in order:
        to_acq(peer).wait_send()
    for d in range(1, n_grp):
        telling(d, g, (g + d) % n_grp).wait_send()
    for k in steps:
        for d, peer in enumerate(others):
            across(g, k, peer, send_x, recv_x, d).wait_send()
        across(g, k, mate, send_c, recv_c, 0).wait_send()
        for d, owner in enumerate(origins):
            across(owner, k, mate, send_c, recv_c, d + 1).wait_send()


def body(tile_slabs, dest_rank, block_slot, shifts, blend_weight, parent_map):
    n_acq, n_grp = lax.axis_size("acq"), lax.axis_size("grp")
    count = tile_slabs.shape[0]
    subs = dest_rank.shape[0]
    blocks = parent_map.shape[0]
    cap = max(2, 2 * count // n_acq)
    depth = n_acq * cap * HZ
    hbm = pl.BlockSpec(memory_space=pltpu.HBM)
    rows = PAIRS * HZ
    dma = pltpu.SemaphoreType.DMA
    n_hi = n_grp // 2
    summed = pl.pallas_call(
        functools.partial(kernel, n_acq, n_grp, cap),
        out_shape=jax.ShapeDtypeStruct((PAR_DEV * 8 * HZ, LANES), jnp.float32),
        in_specs=[hbm] * 6,
        out_specs=pl.BlockSpec(memory_space=pltpu.VMEM),
        scratch_shapes=[
            pltpu.SMEM((1, subs), jnp.int32),
            pltpu.SMEM((1, subs), jnp.int32),
            pltpu.SMEM((1, subs), jnp.float32),
            pltpu.SMEM((3, subs), jnp.float32),
            pltpu.SMEM((1, blocks), jnp.int32),
            pltpu.VMEM((1, subs), jnp.int32),
            pltpu.VMEM((1, subs), jnp.int32),
            pltpu.VMEM((1, subs), jnp.float32),
            pltpu.VMEM((count, BZ, BY * BX), jnp.float32),
            pltpu.VMEM((count, HY, BZ, BX), jnp.float32),
            pltpu.VMEM((count, rows, 2 * BX), jnp.float32),
            pltpu.VMEM((count, rows, 2 * BX), jnp.float32),
            pltpu.VMEM((count + 1, rows, 2 * BX), jnp.float32),
            pltpu.VMEM((count + 1, HZ, BX), jnp.float32),
            pltpu.VMEM((n_acq, cap * HZ, LANES), jnp.float32),
            pltpu.VMEM((n_grp, n_acq, cap * HZ, LANES), jnp.float32),
            pltpu.VMEM((n_grp, HZ, depth), jnp.int32),
            dma((8,)), dma((count,)),
            dma((n_acq,)), dma((n_acq,)),
            dma((max(1, n_hi - 1), n_acq)), dma((n_grp, n_acq)),
            dma((n_hi, n_acq)), dma((n_grp, n_acq)),
            dma((n_grp,)), dma((n_grp,)),
        ],
        compiler_params=pltpu.CompilerParams(
            collective_id=0, has_side_effects=True, vmem_limit_bytes=VMEM_LIMIT * 2**20
        ),
    )(
        tile_slabs, dest_rank.reshape(1, subs), block_slot.reshape(1, subs),
        blend_weight.reshape(1, subs), shifts.T, parent_map.reshape(1, blocks),
    )
    return summed.reshape(PAR_DEV, 8, HZ, LANES)


def solution(mesh):
    placed = (P(("acq", "grp"), None, None), P(), P(), P(), P(), P(("acq", "grp")))
    return jax.shard_map(
        body,
        mesh=mesh,
        in_specs=placed,
        out_specs=P(("acq", "grp"), None, None, None),
        check_vma=False,
    )
```

time: 40.2 us -> 29.2 us (0.73)
  local copies, waits for them, and re-layouts: 7.5 us -> 1.89 us
  other arithmetic: 4.01 us -> 0 us
  Pallas kernels: 28.3 us -> 27.1 us
    reshape x5 -> x0, local copies, waits for them, and re-layouts: 3.08 us -> none  [the longest x1 0.77 us: body(): shifts.reshape(n_acq * n_grp, count, 3)]
    broadcast_in_dim x3 -> x0, local copies, waits for them, and re-layouts: 1.47 us -> none  [the longest x1 1.32 us: body(): parents = jnp.broadcast_to(parent_map[:, None], (blocks, depth))]
    unnamed x1 -> x0, other arithmetic: 1.34 us -> none
    reduce_sum x5 -> x0, other arithmetic: 1.31 us -> none  [the longest x1 0.64 us: body(): order = jnp.sum((here[:, :, None, :] & earlier).astype(jnp.int32), axis=3)]
    pallas_call x1, Pallas kernels: 28.3 us -> 27.1 us  [body(): pl.pallas_call(functools.partial(kernel, n_acq, n_grp, cap), out_shape=ja...]
    concatenate x1 -> x0, other arithmetic: 0.67 us -> none  [body(): scal = jnp.concatenate([offsets, factor[:, None]], axis=1)]
    sub x3 -> x0, other arithmetic: 0.6 us -> none  [the longest x1 0.59 us: body(): count - jnp.sum(jnp.where(send_rows[:, None] == spot[None, :], count - in...]
    unnamed x2 -> x1, local copies, waits for them, and re-layouts: 2.4 us -> 1.89 us
where the time goes in v2:
time: 29.2 us; the launch traced here: 29 us
  Pallas kernels  27.1 us (93%)
  local copies, waits for them, and re-layouts  1.89 us (6%)
    pallas_call x1, Pallas kernels, body(): pl.pallas_call(functools.partial(kernel, n_acq, n_grp, cap), out_shape=ja...  27.1 us
    unnamed x1, local copies, waits for them, and re-layouts  1.89 us

profile of v2, /device:TPU:1, one launch (start us, length us, event | category | flops | bytes accessed | tf_op | source)
XLA Modules:
  0.0 29.0 jit_solution(15173586610654386871)
XLA Ops:
  0.0 27.1 %shard_map.64 = f32[128,1024]{1,0:T(8,128)} custom-call(f32[8,16,4096]{2,1,0:T(8,128)} %tile_hbm.1, s32[1,256]{1,0:T(1,128)} %bitcast.8, s32[1,256]{1,0:T(1,128)} %bitcast.9, f32[1,256]{1,0:T(1,128)} %bitcast.10, f32[3,256]{1,0:T(4,128)} %bitcast.7, s32[1,16]{1,0:T(1,128)} %bitcast.11), custom_call_target="tpu_custom_call" | custom-call | tf_op jit(solution)/shard_map/pallas_call | solution.py:285
  27.1 1.9 %copy.8 = f32[2,8,8,1024]{3,2,1,0:T(8,128)} copy(f32[2,8,8,1024]{3,2,1,0:T(8,128)} %bitcast.6) | data formatting | bytes 1048576

commit v3 on v2

--- a/solution.py
+++ b/solution.py
@@ -169,10 +169,12 @@
             device_id=(peer, g), device_id_type=MESH,
         )
 
-    def across(owner, k, peer, sends, recvs, at):
+    def across(owner, part, peer, sends, recvs, at):
+        first, size = parts[part][1:]
+        rows_ref = gath.at[owner, pl.ds(first, size)]
         return pltpu.make_async_remote_copy(
-            src_ref=gath.at[owner, k], dst_ref=gath.at[owner, k],
-            send_sem=sends.at[at, k], recv_sem=recvs.at[owner, k],
+            src_ref=rows_ref, dst_ref=rows_ref,
+            send_sem=sends.at[at, part], recv_sem=recvs.at[owner, part],
             device_id=(a, peer), device_id_type=MESH,
         )
 
@@ -180,6 +182,14 @@
     order = [flip(a, d, n_acq) for d in partners(n_acq)]
     for peer in order:
         to_acq(peer).start()
+
+    steps = [a] + order
+    parts = []
+    for i, k in enumerate(steps):
+        if i < 2 or n_acq & (n_acq - 1):
+            parts.append(([i], k, 1))
+        elif i % 2 == 1:
+            parts.append(([i - 1, i], (k // 2) * 2, 2))
 
     others = [((hi + d) % n_hi) * 2 + lo for d in range(1, n_hi)]
     origins = [((hi + n_hi - d) % n_hi) * 2 + lo for d in range(1, n_hi)]
@@ -214,8 +224,7 @@
             found = jnp.where(lane // HZ == k * cap + c, parent[0, slots[c]], found)
         return found
 
-    steps = [a] + order
-    forward(a)
+    forward(0)
     named[g] = lax.fori_loop(0, n_acq, name, jnp.zeros((HZ, depth), jnp.int32))
 
     def telling(d, owner, peer):
@@ -240,22 +249,23 @@
             placing, rest, preferred_element_type=jnp.float32
         )
 
-    for i in range(1, n_acq):
-        from_acq(steps[i]).wait_recv()
-        forward(steps[i])
-        relay(steps[i - 1])
+    for part in range(1, len(parts)):
+        for i in parts[part][0]:
+            from_acq(steps[i]).wait_recv()
+        forward(part)
+        relay(part - 1)
     out[...] = place_rows(g)
     for d in range(1, n_grp):
         owner = (g + n_grp - d) % n_grp
         telling(d, owner, owner).wait_recv()
-    for k in steps:
+    for k in range(len(parts)):
         across(mate, k, mate, send_c, recv_c, 0).wait_recv()
     out[...] += place_rows(mate)
-    relay(steps[-1])
+    relay(len(parts) - 1)
     for owner in origins:
         out[...] += place_rows(owner)
     for owner in mates[1:]:
-        for k in steps:
+        for k in range(len(parts)):
             across(owner, k, mate, send_c, recv_c, 0).wait_recv()
         out[...] += place_rows(owner)
 
@@ -263,7 +273,7 @@
         to_acq(peer).wait_send()
     for d in range(1, n_grp):
         telling(d, g, (g + d) % n_grp).wait_send()
-    for k in steps:
+    for k in range(len(parts)):
         for d, peer in enumerate(others):
             across(g, k, peer, send_x, recv_x, d).wait_send()
         across(g, k, mate, send_c, recv_c, 0).wait_send()

time: 29.2 us -> 27.6 us (0.945)
  Pallas kernels: 27.1 us -> 25.3 us
    pallas_call x1, Pallas kernels: 27.1 us -> 25.3 us  [body(): pl.pallas_call(functools.partial(kernel, n_acq, n_grp, cap), out_shape=ja...]
where the time goes in v3:
time: 27.6 us; the launch traced here: 27.2 us
  Pallas kernels  25.3 us (92%)
  local copies, waits for them, and re-layouts  1.89 us (7%)
    pallas_call x1, Pallas kernels, body(): pl.pallas_call(functools.partial(kernel, n_acq, n_grp, cap), out_shape=ja...  25.3 us
    unnamed x1, local copies, waits for them, and re-layouts  1.89 us

profile of v3, /device:TPU:1, one launch (start us, length us, event | category | flops | bytes accessed | tf_op | source)
XLA Modules:
  0.0 27.2 jit_solution(7842429323192950724)
XLA Ops:
  0.0 25.3 %shard_map.64 = f32[128,1024]{1,0:T(8,128)} custom-call(f32[8,16,4096]{2,1,0:T(8,128)} %tile_hbm.1, s32[1,256]{1,0:T(1,128)} %bitcast.8, s32[1,256]{1,0:T(1,128)} %bitcast.9, f32[1,256]{1,0:T(1,128)} %bitcast.10, f32[3,256]{1,0:T(4,128)} %bitcast.7, s32[1,16]{1,0:T(1,128)} %bitcast.11), custom_call_target="tpu_custom_call" | custom-call | tf_op jit(solution)/shard_map/pallas_call | solution.py:295
  25.3 1.9 %copy.8 = f32[2,8,8,1024]{3,2,1,0:T(8,128)} copy(f32[2,8,8,1024]{3,2,1,0:T(8,128)} %bitcast.6) | data formatting | bytes 1048576
